TPU v7x, 32 devices: a whole 2x2x4 slice. The times are simulated.
32 devices in a mesh: groups: 2 (over x), prompt: 8 (over z, y), resp: 2 (over core).
Axes of the slice: x: 2, y: 2, z: 4, core: 2. Of those that a mesh axis runs over, the one named last changes fastest.
Arguments:
- queries: bfloat16 [16, 512, 1024], P(('groups', 'prompt'), 'resp'), parts along dimension 0, may hold values from -4096 to 4096
- grad_out: bfloat16 [16, 512, 1024], P(('groups', 'prompt'), 'resp'), parts along dimension 0, may hold values from -48 to 48
- keys_resp: bfloat16 [16, 512, 128], P(('groups', 'prompt'), 'resp'), parts along dimension 0, may hold values from -6 to 6
- values_resp: bfloat16 [16, 512, 128], P(('groups', 'prompt'), 'resp'), parts along dimension 0, may hold values from -6 to 6
- keys_prefix: bfloat16 [1024, 128], P(('groups', 'prompt')), parts along dimension 0, may hold values from -32 to 32
- values_prefix: bfloat16 [1024, 128], P(('groups', 'prompt')), parts along dimension 0, may hold values from -6 to 6
- lengths: int32 [16], P(('groups', 'prompt')), parts along dimension 0, may hold values from 1 to 512, as said below
- block_plan: int32 [16, 4], P(('groups', 'prompt'), 'resp'), parts along dimension 0, may hold values from 0 to 3, as said below
Outputs:
- query_grads: float32 [16, 512, 1024], P(('groups', 'prompt'), 'resp'), parts along dimension 0
- prefix_keygrad: float32 [1024, 128], P(('groups', 'prompt', 'resp')), parts along dimension 0
- prefix_valgrad: float32 [1024, 128], P(('groups', 'prompt', 'resp')), parts along dimension 0
- reply_keygrad: float32 [16, 512, 128], P(('groups', 'prompt'), 'resp'), parts along dimension 0
- reply_valgrad: float32 [16, 512, 128], P(('groups', 'prompt'), 'resp'), parts along dimension 0
There are 2 independent parts, one for each index of `groups`. A program takes and returns all parts, laid end to end along the dimension named above; each array names one. Nothing has to cross between parts.
Inputs may be any that keep to these rules, and one draw needn't show every extreme that they name: `lengths`: one response has exactly 512 live positions. `block_plan`: each row is a permutation of 0 to 3; for every m, blocks 2 * m and 2 * m + 1 stand in different halves of the row.
All inputs are finite; a program needn't handle non-finite values.
Results may differ from a plain program's by a relative error of at most 0.0029.
Values may be sent and summed in bfloat16 or wider, within the bound.
No kernel may reach another device: no remote copies, remote signals or barrier semaphores. Data moves between devices by JAX's collectives and lax.ppermute only.
A program may use at most 64 MiB of HBM per device.

v0:
```python
import jax
import jax.numpy as jnp
from jax import lax
from jax.sharding import PartitionSpec as P

RBLK = 128


def block_terms(
    query_block, grad_block, first_row, length, all_keys, all_values, prefix_len, head_count
):
    row_count = query_block.shape[0]
    head_width = all_keys.shape[1]
    key_count = all_keys.shape[0]
    score_scale = head_width ** (-0.5)
    positions = first_row + jnp.arange(row_count, dtype=jnp.int32)
    key_index = jnp.arange(key_count, dtype=jnp.int32)
    relative = key_index - prefix_len
    visible = (key_index[None, :] < prefix_len) | (relative[None, :] <= positions[:, None]) & (
        relative[None, :] < length
    )
    live_rows = positions < length
    query_heads = query_block.reshape(row_count, head_count, head_width)
    grad_heads = jnp.where(
        live_rows[:, None, None],
        grad_block.reshape(row_count, head_count, head_width),
        jnp.zeros((), jnp.bfloat16),
    )
    half_heads = head_count // 2

    def active_block(unused):
        grad_parts = []
        grad_k = jnp.zeros((key_count, head_width), jnp.float32)
        grad_v = jnp.zeros((key_count, head_width), jnp.float32)
        for group_index in range(2):
            query_part = query_heads[:, group_index * half_heads : (group_index + 1) * half_heads]
            grad_part = grad_heads[:, group_index * half_heads : (group_index + 1) * half_heads]
            scores = (
                jnp.einsum("rhd,kd->rhk", query_part, all_keys, preferred_element_type=jnp.float32)
                * score_scale
            )
            scores = jnp.where(visible[:, None, :], scores, -jnp.inf)
            row_max = jnp.max(scores, -1, keepdims=True)
            exponent = jnp.exp(scores - row_max)
            weights = exponent / jnp.sum(exponent, -1, keepdims=True)
            grad_weight = jnp.einsum(
                "rhd,kd->rhk", grad_part, all_values, preferred_element_type=jnp.float32
            )
            row_inner = jnp.sum(weights * grad_weight, -1, keepdims=True)
            grad_score = (weights * (grad_weight - row_inner)).astype(jnp.bfloat16)
            rounded_weights = weights.astype(jnp.bfloat16)
            grad_query = (
                jnp.einsum("rhk,kd->rhd", grad_score, all_keys, preferred_element_type=jnp.float32)
                * score_scale
            )
            grad_parts.append(grad_query)
            grad_k = (
                grad_k
                + jnp.einsum(
                    "rhk,rhd->kd", grad_score, query_part, preferred_element_type=jnp.float32
                )
                * score_scale
            )
            grad_v = grad_v + jnp.einsum(
                "rhk,rhd->kd", rounded_weights, grad_part, preferred_element_type=jnp.float32
            )
        joined = jnp.concatenate(grad_parts, 1).reshape(row_count, head_count * head_width)
        return (joined, grad_k, grad_v)

    def empty_block(unused):
        return (
            jnp.zeros((row_count, head_count * head_width), jnp.float32),
            jnp.zeros((key_count, head_width), jnp.float32),
            jnp.zeros((key_count, head_width), jnp.float32),
        )

    return lax.cond(first_row < length, active_block, empty_block, 0)


def local(
    queries, grad_out, keys_resp, values_resp, keys_prefix, values_prefix, lengths, block_plan
):
    core_count = lax.axis_size("resp")
    slot_count = queries.shape[1]
    head_width = keys_prefix.shape[1]
    full_width = queries.shape[2]
    head_count = full_width // head_width
    block_count = slot_count // RBLK
    total_blocks = block_count * core_count
    length = lengths[0]
    prefix_keys, prefix_values = (
        lax.all_gather(keys_prefix, "prompt", axis=0, tiled=True),
        lax.all_gather(values_prefix, "prompt", axis=0, tiled=True),
    )
    prefix_len = prefix_keys.shape[0]
    plan_row = block_plan[0]
    query_all, grad_all, reply_keys, reply_values = (
        lax.all_gather(queries, "resp", axis=1, tiled=True),
        lax.all_gather(grad_out, "resp", axis=1, tiled=True),
        lax.all_gather(keys_resp, "resp", axis=1, tiled=True),
        lax.all_gather(values_resp, "resp", axis=1, tiled=True),
    )
    query_work = jnp.take(query_all.reshape(total_blocks, RBLK, full_width), plan_row, axis=0)
    grad_work = jnp.take(grad_all.reshape(total_blocks, RBLK, full_width), plan_row, axis=0)
    starts = plan_row * RBLK
    all_keys = jnp.concatenate([prefix_keys, reply_keys[0]], 0)
    all_values = jnp.concatenate([prefix_values, reply_values[0]], 0)

    def advance(totals, block_item):
        query_block, grad_block, first_row = block_item
        grad_query, grad_k, grad_v = block_terms(
            query_block, grad_block, first_row, length, all_keys, all_values, prefix_len, head_count
        )
        return ((totals[0] + grad_k, totals[1] + grad_v), grad_query)

    zeros = jnp.zeros(all_keys.shape, jnp.float32)
    totals, grad_blocks = lax.scan(advance, (zeros, zeros), (query_work, grad_work, starts))
    local_grads = grad_blocks.reshape(1, slot_count, full_width)
    key_total, value_total = totals
    reply_keygrad, reply_valgrad = (
        lax.psum_scatter(key_total[prefix_len:][None], "resp", scatter_dimension=1, tiled=True),
        lax.psum_scatter(value_total[prefix_len:][None], "resp", scatter_dimension=1, tiled=True),
    )
    prefix_k = key_total[:prefix_len]
    prefix_v = value_total[:prefix_len]
    prefix_keygrad, prefix_valgrad = (
        lax.psum_scatter(prefix_k, ("prompt", "resp"), scatter_dimension=0, tiled=True),
        lax.psum_scatter(prefix_v, ("prompt", "resp"), scatter_dimension=0, tiled=True),
    )
    return (local_grads, prefix_keygrad, prefix_valgrad, reply_keygrad, reply_valgrad)


def solution(mesh):
    placed = (
        P(("groups", "prompt"), "resp", None),
        P(("groups", "prompt"), "resp", None),
        P(("groups", "prompt"), "resp", None),
        P(("groups", "prompt"), "resp", None),
        P(("groups", "prompt"), None),
        P(("groups", "prompt"), None),
        P(("groups", "prompt")),
        P(("groups", "prompt"), "resp"),
    )
    return jax.shard_map(
        local,
        mesh=mesh,
        in_specs=placed,
        out_specs=(
            P(("groups", "prompt"), "resp", None),
            P(("groups", "prompt", "resp"), None),
            P(("groups", "prompt", "resp"), None),
            P(("groups", "prompt"), "resp", None),
            P(("groups", "prompt"), "resp", None),
        ),
        check_vma=False,
    )
```

profile of v0, /device:TPU:0, one launch (start us, length us, event | category | flops | bytes accessed | tf_op | source)
XLA Modules:
  0.0 276.5 jit_solution(17285941282429215589)
XLA Ops:
  7.2 0.0 all-gather.5.cloned.1.call-start
  7.2 0.7 all-gather.5.cloned.1.call-update
  7.9 0.0 all-gather.3.cloned.1.call-start
  8.0 0.7 all-gather.3.cloned.1.call-update
  8.7 0.0 reduce-scatter.5.cloned.1.call-start
  8.8 2.2 all_gather.20
  11.0 32.4 %all_gather.19 = bf16[512,128]{1,0:T(8,128)(2,1)S(1)} all-gather(bf16[64,128]{1,0:T(8,128)(2,1)} %param.18), channel_id=1, replica_groups=mesh['groups'=2,'prompt'=8,'resp'=2] {'prompt'}, dimensions={0}, use_global_device_ids=true | all-gather | bytes 147456 | tf_op jit(solution)/shard_map/all_gather | solution.py:92
  43.4 0.1 copy.58
  43.6 1.9 all_gather.23
  45.5 30.5 %all_gather.22 = bf16[512,128]{1,0:T(8,128)(2,1)S(1)} all-gather(bf16[64,128]{1,0:T(8,128)(2,1)S(1)} %copy-done.2), channel_id=1, replica_groups=mesh['groups'=2,'prompt'=8,'resp'=2] {'prompt'}, dimensions={0}, use_global_device_ids=true | all-gather | bytes 147456 | tf_op jit(solution)/shard_map/all_gather | solution.py:93
  76.0 0.7 pad_maximum_fusion.2
  76.8 1.8 gather_fusion.1
  78.6 0.0 all-gather.3.cloned.1.call-done
  78.6 1.8 gather_fusion
  80.4 0.2 broadcast_select_fusion.1
  80.6 1.0 copy.59
  81.6 1.0 copy.57
  82.6 14.9 %while.17 = (s32[]{:T(128)}, f32[1024,128]{1,0:T(8,128)}, f32[1024,128]{1,0:T(8,128)}, f32[2,128,1024]{2,1,0:T(8,128)}, s32[2]{0:T(128)S(1)}, /*index=5*/s32[]{:...) while((s32[]{:T(128)}, f32[1024,128]{1,0:T(8,128)}, ...), condition=%wide.region_9.11_spmd.clone, body=%wide.region_0.10_spmd.clone.sunk | while | flops 1629102464 | bytes 53665412 | solution.py:117
  82.6 0.6 dynamic_slice.32
  84.5 1.8 conditional.3
  84.5 0.8 broadcast.91.clone
  85.4 0.9 broadcast.91
  86.3 2.4 select_add_fusion.3
  88.7 0.2 copy.74
  88.9 0.0 copy-done.3
  88.9 0.0 copy-start.4
  88.9 1.0 copy-done.4
  89.9 0.6 dynamic_slice.32
  91.8 1.8 conditional.3
  91.8 0.8 broadcast.91.clone
  92.7 0.9 broadcast.91
  93.6 2.7 select_add_fusion.3
  96.3 0.2 copy.74
  96.5 0.0 copy-start.4
  96.6 1.0 copy-done.4
  97.5 1.9 slice_bitcast_fusion.1
  99.4 0.0 reduce-scatter.5.cloned.1.call-update
  99.4 0.0 reduce-scatter.7.cloned.1.call-start
  99.4 1.9 slice_bitcast_fusion
  101.3 0.0 reduce-scatter.7.cloned.1.call-update
  101.3 0.0 reduce-scatter.9.cloned.1.call-start
  101.4 0.5 reduce-scatter.9.cloned.1.call-update
  101.9 0.0 reduce-scatter.11.cloned.1.call-start
  102.0 0.5 reduce-scatter.11.cloned.1.call-update
  102.5 87.4 %reduce-scatter.5.cloned.1.call-done = f32[32,128]{1,0:T(8,128)} async-done(((f32[512,128]{1,0:T(8,128)}), f32[32,128]{1,0:T(8,128)}) %reduce-scatter.5.cloned.1.call-update) | async-done | bytes 16400 | tf_op jit(solution)/shard_map/reduce_scatter | solution.py:127
  189.9 58.7 %reduce-scatter.7.cloned.1.call-done = f32[32,128]{1,0:T(8,128)} async-done(((f32[512,128]{1,0:T(8,128)}), f32[32,128]{1,0:T(8,128)}) %reduce-scatter.7.cloned.1.call-update) | async-done | bytes 16400 | tf_op jit(solution)/shard_map/reduce_scatter | solution.py:128
  248.7 9.4 %reduce-scatter.9.cloned.1.call-done = f32[1,256,128]{2,1,0:T(8,128)} async-done(((f32[1,512,128]{2,1,0:T(8,128)}), f32[1,256,128]{2,1,0:T(8,128)}) %reduce-scatter.9.cloned.1.call-update) | async-done | bytes 131088 | tf_op jit(solution)/shard_map/reduce_scatter | solution.py:121
  258.1 11.5 %reduce-scatter.11.cloned.1.call-done = f32[1,256,128]{2,1,0:T(8,128)} async-done(((f32[1,512,128]{2,1,0:T(8,128)}), f32[1,256,128]{2,1,0:T(8,128)}) %reduce-scatter.11.cloned.1.call-update) | async-done | bytes 131088 | tf_op jit(solution)/shard_map/reduce_scatter | solution.py:122
  (27 shorter events, 0.3 us)
Async XLA Ops:
  7.2 36.4 %copy-start.1 = (bf16[1,256,128]{2,1,0:T(8,128)(2,1)S(1)}, bf16[1,256,128]{2,1,0:T(8,128)(2,1)}, u32[]{:S(2)}) copy-start(bf16[1,256,128]{2,1,0:T(8,128)(2,1)} %param.17) | copy-start | bytes 196612
  7.2 38.3 %copy-start.2 = (bf16[64,128]{1,0:T(8,128)(2,1)S(1)}, bf16[64,128]{1,0:T(8,128)(2,1)}, u32[]{:S(2)}) copy-start(bf16[64,128]{1,0:T(8,128)(2,1)} %param.19) | copy-start | bytes 49156
  7.2 68.8 %copy-start.5 = (s32[1,2]{1,0:T(1,128)S(1)}, s32[1,2]{1,0:T(1,128)}, u32[]{:S(2)}) copy-start(s32[1,2]{1,0:T(1,128)} %param.21) | copy-start | bytes 28
  7.2 69.6 %all-gather.5.cloned.1.call-start = ((), (), s32[]{:S(2)}) async-start(), calls=%async_computation.5 | async-start | bytes 1572864 | tf_op jit(solution)/shard_map/all_gather | solution.py:99
  7.9 70.7 %all-gather.3.cloned.1.call-start = ((), (), s32[]{:S(2)}) async-start(), calls=%async_computation.4 | async-start | bytes 1572864 | tf_op jit(solution)/shard_map/all_gather | solution.py:98
  8.7 181.2 %reduce-scatter.5.cloned.1.call-start = ((), (), s32[]{:S(2)}) async-start(), calls=%async_computation.6 | async-start | bytes 278528 | tf_op jit(solution)/shard_map/reduce_scatter | solution.py:127
  86.3 2.6 copy-start.3
  88.9 1.0 copy-start.4
  93.6 2.9 %copy-start.3 = (f32[2,128,1024]{2,1,0:T(8,128)S(1)}, f32[2,128,1024]{2,1,0:T(8,128)}, u32[]{:S(2)}) copy-start(f32[2,128,1024]{2,1,0:T(8,128)} %get-tuple-element.493) | copy-start | bytes 3145732 | tf_op jit(solution)/shard_map/while
  96.5 1.0 copy-start.4
  99.4 149.3 %reduce-scatter.7.cloned.1.call-start = ((), (), s32[]{:S(2)}) async-start(), calls=%async_computation.7 | async-start | bytes 278528 | tf_op jit(solution)/shard_map/reduce_scatter | solution.py:128
  101.3 156.7 %reduce-scatter.9.cloned.1.call-start = ((), (), s32[]{:S(2)}) async-start(), calls=%async_computation.8 | async-start | bytes 393216 | tf_op jit(solution)/shard_map/reduce_scatter | solution.py:121
  101.9 167.7 %reduce-scatter.11.cloned.1.call-start = ((), (), s32[]{:S(2)}) async-start(), calls=%async_computation.9 | async-start | bytes 393216 | tf_op jit(solution)/shard_map/reduce_scatter | solution.py:122
Sparse Core Ops, SparseCore 0:
  9.5 11.7 all-gather.4
  22.9 10.1 all-gather.2
  99.5 90.3 reduce-scatter.4
  193.9 54.7 reduce-scatter.6
  251.3 6.7 reduce-scatter.8
  260.7 8.8 reduce-scatter.10
where the time goes:
time: 277 us; the launch traced here: 276 us
  waiting for transfers between devices  170 us (61%)
  blocking collectives  67.1 us (24%)
  local copies, waits for them, and re-layouts  16.6 us (6%)
  between operations  14.2 us (5%)
  other arithmetic  6.03 us (2%)
    reduce_scatter x1, waiting for transfers between devices, local(): lax.psum_scatter(prefix_k, ('prompt', 'resp'), scatter_dimension=0, tiled...  87.4 us
    reduce_scatter x1, waiting for transfers between devices, local(): lax.psum_scatter(prefix_v, ('prompt', 'resp'), scatter_dimension=0, tiled...  58.7 us
    all_gather x1, blocking collectives, local(): lax.all_gather(keys_prefix, 'prompt', axis=0, tiled=True)  32.4 us
    all_gather x1, blocking collectives, local(): lax.all_gather(values_prefix, 'prompt', axis=0, tiled=True)  30.5 us
    reduce_scatter x1, waiting for transfers between devices, local(): lax.psum_scatter(value_total[prefix_len:][None], 'resp', scatter_dimensio...  11.5 us
    reduce_scatter x1, waiting for transfers between devices, local(): lax.psum_scatter(key_total[prefix_len:][None], 'resp', scatter_dimension=...  9.41 us
  transfers between devices with their start and end apart: 6, of which 4 were waited for; matrix products, arithmetic and copies ran while one was open for 2% of the time, Pallas kernels for 0%

commit v1 on v0

--- a/solution.py
+++ b/solution.py
@@ -4,6 +4,11 @@
 from jax.sharding import PartitionSpec as P
 
 RBLK = 128
+
+
+def exchange_gather(block, name, dim):
+    stack = jnp.stack([block] * lax.axis_size(name))
+    return jnp.concatenate(lax.all_to_all(stack, name, 0, 0), axis=dim)
 
 
 def block_terms(
@@ -89,7 +94,7 @@
     total_blocks = block_count * core_count
     length = lengths[0]
     prefix_keys, prefix_values = (
-        lax.all_gather(keys_prefix, "prompt", axis=0, tiled=True),
+        exchange_gather(keys_prefix, "prompt", 0),
         lax.all_gather(values_prefix, "prompt", axis=0, tiled=True),
     )
     prefix_len = prefix_keys.shape[0]

time: 277 us -> 255 us (0.921)
  blocking collectives: 67.1 us -> 35.2 us
  starting transfers between devices: 0.23 us -> 7.54 us
    all_gather x1 -> x0, blocking collectives: 32.4 us -> none  [local(): lax.all_gather(keys_prefix, 'prompt', axis=0, tiled=True)]
    all_to_all x0 -> x1, starting transfers between devices: none -> 7.31 us  [exchange_gather(): return jnp.concatenate(lax.all_to_all(stack, name, 0, 0), axis=dim)]
  transfers between devices with their start and end apart: 6 -> 7, of which waited for: 4 -> 4; matrix products, arithmetic and copies ran while one was open for 2% -> 3% of each run, Pallas kernels for 0% -> 0%
where the time goes in v1:
time: 255 us; the launch traced here: 254 us
  waiting for transfers between devices  169 us (66%)
  blocking collectives  35.2 us (14%)
  local copies, waits for them, and re-layouts  18 us (7%)
  between operations  14.2 us (6%)
  starting transfers between devices  7.54 us (3%)
  other arithmetic  6.68 us (3%)
  loops' own time  2.75 us (1%)
    reduce_scatter x1, waiting for transfers between devices, local(): lax.psum_scatter(prefix_k, ('prompt', 'resp'), scatter_dimension=0, tiled...  87.2 us
    reduce_scatter x1, waiting for transfers between devices, local(): lax.psum_scatter(prefix_v, ('prompt', 'resp'), scatter_dimension=0, tiled...  58.7 us
    all_gather x1, blocking collectives, local(): lax.all_gather(values_prefix, 'prompt', axis=0, tiled=True)  31.2 us
    reduce_scatter x1, waiting for transfers between devices, local(): lax.psum_scatter(value_total[prefix_len:][None], 'resp', scatter_dimensio...  11.5 us
    reduce_scatter x1, waiting for transfers between devices, local(): lax.psum_scatter(key_total[prefix_len:][None], 'resp', scatter_dimension=...  9.47 us
    all_to_all x1, starting transfers between devices, exchange_gather(): return jnp.concatenate(lax.all_to_all(stack, name, 0, 0), axis=dim)  7.31 us
  transfers between devices with their start and end apart: 7, of which 4 were waited for; matrix products, arithmetic and copies ran while one was open for 3% of the time, Pallas kernels for 0%

profile of v1, /device:TPU:0, one launch (start us, length us, event | category | flops | bytes accessed | tf_op | source)
XLA Modules:
  0.0 253.9 jit_solution(14914734943026473867)
XLA Ops:
  7.2 0.0 all-gather.5.cloned.1.call-start
  7.2 0.7 all-gather.5.cloned.1.call-update
  7.9 0.0 all-gather.3.cloned.1.call-start
  8.0 0.7 all-gather.3.cloned.1.call-update
  8.7 1.4 stack.2
  10.1 7.3 %all-to-all-start = ((bf16[8,64,128]{2,1,0:T(8,128)(2,1)}), bf16[8,64,128]{2,1,0:T(8,128)(2,1)S(1)}, u32[]{:S(2)}, u32[]{:S(2)}) async-start(bf16[8,64,128]{2,1,0:T(8,128)(2,1)} %stack.2), calls=%async_computation | async-start | bytes 262144 | tf_op jit(solution)/shard_map/all_to_all | solution.py:11
  17.4 0.0 reduce-scatter.5.cloned.1.call-start
  17.4 2.1 all_gather.19
  19.5 31.2 %all_gather.18 = bf16[512,128]{1,0:T(8,128)(2,1)S(1)} all-gather(bf16[64,128]{1,0:T(8,128)(2,1)} %param.19), channel_id=1, replica_groups=mesh['groups'=2,'prompt'=8,'resp'=2] {'prompt'}, dimensions={0}, use_global_device_ids=true | all-gather | bytes 147456 | tf_op jit(solution)/shard_map/all_gather | solution.py:98
  50.8 0.7 compare_select_fusion
  51.4 0.7 pad_maximum_fusion.2
  52.2 1.9 all_gather.16
  54.1 0.1 copy.43
  54.3 0.0 all-gather.5.cloned.1.call-done
  54.3 1.8 gather_fusion.1
  56.1 0.0 all-gather.3.cloned.1.call-done
  56.1 1.8 gather_fusion
  57.9 0.2 broadcast_select_fusion.1
  58.1 1.0 copy.44
  59.1 1.0 copy.42
  60.1 14.9 %while.17 = (s32[]{:T(128)}, f32[1024,128]{1,0:T(8,128)}, f32[1024,128]{1,0:T(8,128)}, f32[2,128,1024]{2,1,0:T(8,128)}, s32[2]{0:T(128)S(1)}, /*index=5*/s32[]{:...) while((s32[]{:T(128)}, f32[1024,128]{1,0:T(8,128)}, ...), condition=%wide.region_9.11_spmd.clone, body=%wide.region_0.10_spmd.clone.sunk | while | flops 1629102464 | bytes 53665412 | solution.py:122
  60.1 0.6 dynamic_slice.32
  62.0 1.8 conditional.3
  62.0 0.8 broadcast.93.clone
  62.9 0.9 broadcast.93
  63.8 2.4 select_add_fusion.3
  66.2 0.2 copy.59
  66.5 1.0 copy-done.3
  67.4 0.6 dynamic_slice.32
  69.3 1.8 conditional.3
  69.4 0.8 broadcast.93.clone
  70.2 0.9 broadcast.93
  71.1 2.7 %select_add_fusion.3 = (f32[1024,128]{1,0:T(8,128)}, f32[1024,128]{1,0:T(8,128)}) fusion(f32[1024,128]{1,0:T(8,128)} %get-tuple-element.467, f32[1024,128]{1,0:T(8,128)} %get-tuple-element.492, pred[]{:T(512)S(6)} %compare.3, f32[1024,128]{1,0:T(8,128)} %get-tuple-element.468, f32[1024,128]{1,0:T(8,128)} %get-tuple-element.491), kind=kLoop, calls=%fused_computation.61.clone.1 | loop fusion | flops 524288 | bytes 3145729 | tf_op jit(solution)/shard_map/while/body/eval_jaxpr/add | solution.py:119
  73.8 0.2 copy.59
  74.1 1.0 copy-done.3
  75.0 1.9 slice_bitcast_fusion.1
  76.9 0.0 reduce-scatter.5.cloned.1.call-update
  76.9 0.0 reduce-scatter.7.cloned.1.call-start
  77.0 1.9 slice_bitcast_fusion
  78.8 0.0 reduce-scatter.7.cloned.1.call-update
  78.9 0.0 reduce-scatter.9.cloned.1.call-start
  78.9 0.5 reduce-scatter.9.cloned.1.call-update
  79.5 0.0 reduce-scatter.11.cloned.1.call-start
  79.5 0.5 reduce-scatter.11.cloned.1.call-update
  80.0 87.2 %reduce-scatter.5.cloned.1.call-done = f32[32,128]{1,0:T(8,128)} async-done(((f32[512,128]{1,0:T(8,128)}), f32[32,128]{1,0:T(8,128)}) %reduce-scatter.5.cloned.1.call-update) | async-done | bytes 16400 | tf_op jit(solution)/shard_map/reduce_scatter | solution.py:132
  167.3 58.7 %reduce-scatter.7.cloned.1.call-done = f32[32,128]{1,0:T(8,128)} async-done(((f32[512,128]{1,0:T(8,128)}), f32[32,128]{1,0:T(8,128)}) %reduce-scatter.7.cloned.1.call-update) | async-done | bytes 16400 | tf_op jit(solution)/shard_map/reduce_scatter | solution.py:133
  226.0 9.5 %reduce-scatter.9.cloned.1.call-done = f32[1,256,128]{2,1,0:T(8,128)} async-done(((f32[1,512,128]{2,1,0:T(8,128)}), f32[1,256,128]{2,1,0:T(8,128)}) %reduce-scatter.9.cloned.1.call-update) | async-done | bytes 131088 | tf_op jit(solution)/shard_map/reduce_scatter | solution.py:126
  235.5 11.5 %reduce-scatter.11.cloned.1.call-done = f32[1,256,128]{2,1,0:T(8,128)} async-done(((f32[1,512,128]{2,1,0:T(8,128)}), f32[1,256,128]{2,1,0:T(8,128)}) %reduce-scatter.11.cloned.1.call-update) | async-done | bytes 131088 | tf_op jit(solution)/shard_map/reduce_scatter | solution.py:127
  (27 shorter events, 0.3 us)
Async XLA Ops:
  7.2 46.9 %copy-start.4 = (s32[1,2]{1,0:T(1,128)S(1)}, s32[1,2]{1,0:T(1,128)}, u32[]{:S(2)}) copy-start(s32[1,2]{1,0:T(1,128)} %param.21) | copy-start | bytes 28
  7.2 45.0 %copy-start.1 = (bf16[1,256,128]{2,1,0:T(8,128)(2,1)S(1)}, bf16[1,256,128]{2,1,0:T(8,128)(2,1)}, u32[]{:S(2)}) copy-start(bf16[1,256,128]{2,1,0:T(8,128)(2,1)} %param.16) | copy-start | bytes 196612
  7.2 47.1 %all-gather.5.cloned.1.call-start = ((), (), s32[]{:S(2)}) async-start(), calls=%async_computation.6 | async-start | bytes 1572864 | tf_op jit(solution)/shard_map/all_gather | solution.py:104
  7.9 48.2 %all-gather.3.cloned.1.call-start = ((), (), s32[]{:S(2)}) async-start(), calls=%async_computation.5 | async-start | bytes 1572864 | tf_op jit(solution)/shard_map/all_gather | solution.py:103
  10.1 44.0 %all-to-all-start = ((bf16[8,64,128]{2,1,0:T(8,128)(2,1)}), bf16[8,64,128]{2,1,0:T(8,128)(2,1)S(1)}, u32[]{:S(2)}, u32[]{:S(2)}) async-start(bf16[8,64,128]{2,1,0:T(8,128)(2,1)} %stack.2), calls=%async_computation | async-start | bytes 262144 | tf_op jit(solution)/shard_map/all_to_all | solution.py:11
  17.4 149.9 %reduce-scatter.5.cloned.1.call-start = ((), (), s32[]{:S(2)}) async-start(), calls=%async_computation.7 | async-start | bytes 278528 | tf_op jit(solution)/shard_map/reduce_scatter | solution.py:132
  63.8 2.6 %copy-start.2 = (f32[2,128,1024]{2,1,0:T(8,128)S(1)}, f32[2,128,1024]{2,1,0:T(8,128)}, u32[]{:S(2)}) copy-start(f32[2,128,1024]{2,1,0:T(8,128)} %get-tuple-element.493) | copy-start | bytes 3145732 | tf_op jit(solution)/shard_map/while
  66.4 1.0 copy-start.3
  71.1 2.9 %copy-start.2 = (f32[2,128,1024]{2,1,0:T(8,128)S(1)}, f32[2,128,1024]{2,1,0:T(8,128)}, u32[]{:S(2)}) copy-start(f32[2,128,1024]{2,1,0:T(8,128)} %get-tuple-element.493) | copy-start | bytes 3145732 | tf_op jit(solution)/shard_map/while
  74.1 1.0 copy-start.3
  76.9 149.1 %reduce-scatter.7.cloned.1.call-start = ((), (), s32[]{:S(2)}) async-start(), calls=%async_computation.8 | async-start | bytes 278528 | tf_op jit(solution)/shard_map/reduce_scatter | solution.py:133
  78.9 156.6 %reduce-scatter.9.cloned.1.call-start = ((), (), s32[]{:S(2)}) async-start(), calls=%async_computation.9 | async-start | bytes 393216 | tf_op jit(solution)/shard_map/reduce_scatter | solution.py:126
  79.5 167.6 %reduce-scatter.11.cloned.1.call-start = ((), (), s32[]{:S(2)}) async-start(), calls=%async_computation.10 | async-start | bytes 393216 | tf_op jit(solution)/shard_map/reduce_scatter | solution.py:127
Sparse Core Ops, SparseCore 0:
  9.5 11.7 all-gather.4
  22.9 10.1 all-gather.2
  77.0 90.1 reduce-scatter.4
  171.2 54.7 reduce-scatter.6
  228.6 6.7 reduce-scatter.8
  238.1 8.8 reduce-scatter.10
